TPU v7x, 32 devices: a whole 2x2x4 slice. The times are simulated.
32 devices in a mesh: dp: 4 (over z), sp: 8 (over y, x, core).
Axes of the slice: x: 2, y: 2, z: 4, core: 2. Of those that a mesh axis runs over, the one named last changes fastest.
Arguments:
- x_prompt: bfloat16 [48, 1024, 2048], P('dp', 'sp'), parts along dimension 0
- ln_attn_w: float32 [2048], replicated
- ln_attn_b: float32 [2048], replicated
- ln_mlp_w: float32 [2048], replicated
- ln_mlp_b: float32 [2048], replicated
- w_qkv: bfloat16 [2048, 16, 3, 128], replicated
- w_out: bfloat16 [2048, 2048], replicated
- w_up: bfloat16 [2048, 8192], replicated
- w_down: bfloat16 [8192, 2048], replicated
Outputs:
- output 1: bfloat16 [48, 1024, 2048], P('dp', 'sp'), parts along dimension 0
- output 2: bfloat16 [48, 16, 1024, 128], P('dp', 'sp'), parts along dimension 0
- output 3: bfloat16 [48, 16, 1024, 128], P('dp', 'sp'), parts along dimension 0
There are 4 independent parts. A program takes and returns all parts, laid end to end along the dimension named above; an argument that names none is the same for every part.
All inputs are finite; a program needn't handle non-finite values.
Results may differ from a plain program's by a relative error of at most 0.0040455.
Values are sent between devices in bfloat16 or wider.
A program may use at most 1 GiB of HBM per device.

v0:
```python
import jax
import jax.numpy as jnp
from jax import lax
from jax.sharding import PartitionSpec as P, NamedSharding

LN_EPS = 1e-5
ROPE_BASE = 10000.0


def layer_norm(x_rows, ln_gain, ln_bias):
    x_f32 = x_rows.astype(jnp.float32)
    row_mean = jnp.mean(x_f32, axis=-1, keepdims=True)
    row_var = jnp.mean(jnp.square(x_f32 - row_mean), axis=-1, keepdims=True)
    return ((x_f32 - row_mean) * lax.rsqrt(row_var + LN_EPS) * ln_gain + ln_bias).astype(jnp.bfloat16)


def rope_tables(positions, head_dim):
    half_dim = head_dim // 2
    inv_freq = ROPE_BASE ** (-2.0 * jnp.arange(half_dim, dtype=jnp.float32) / head_dim)
    angles = positions.astype(jnp.float32)[:, None] * inv_freq[None, :]
    return jnp.cos(angles), jnp.sin(angles)


def rotary(t_in, cos_t, sin_t):
    half_dim = t_in.shape[-1] // 2
    t_f32 = t_in.astype(jnp.float32)
    low_half = t_f32[..., :half_dim]
    high_half = t_f32[..., half_dim:]
    return jnp.concatenate([low_half * cos_t - high_half * sin_t, high_half * cos_t + low_half * sin_t], axis=-1).astype(jnp.bfloat16)


def solution(mesh):
    seq_shards = mesh.shape["sp"]
    act_spec = P("dp", "sp", None)
    cache_spec = P("dp", "sp", None, None)
    rep_spec = P()

    def local_layer(x_blk, ln_attn_w, ln_attn_b, ln_mlp_w, ln_mlp_b, w_qkv, w_out, w_up, w_down):
        n_batch = x_blk.shape[0]
        seq_dev = x_blk.shape[1]
        group_size = w_qkv.shape[2] - 2
        head_dim = w_qkv.shape[3]
        shard_idx = lax.axis_index("sp")
        q_pos = shard_idx * seq_dev + jnp.arange(seq_dev)
        k_pos = jnp.arange(seq_shards * seq_dev)
        h_attn = layer_norm(x_blk, ln_attn_w, ln_attn_b)
        h_mlp = layer_norm(x_blk, ln_mlp_w, ln_mlp_b)
        qkv_all = jnp.einsum("bsd,dkgh->bskgh", h_attn, w_qkv, preferred_element_type=jnp.float32).astype(jnp.bfloat16)
        cos_t, sin_t = rope_tables(q_pos, head_dim)
        q_rot = rotary(qkv_all[:, :, :, :group_size], cos_t[:, None, None], sin_t[:, None, None])
        k_rot = rotary(qkv_all[:, :, :, group_size], cos_t[:, None], sin_t[:, None])
        v_loc = qkv_all[:, :, :, group_size + 1]
        k_full = lax.all_gather(k_rot, "sp", axis=1, tiled=True)
        v_full = lax.all_gather(v_loc, "sp", axis=1, tiled=True)
        scores = jnp.einsum("bskgh,btkh->bkgst", q_rot, k_full, preferred_element_type=jnp.float32) * head_dim ** -0.5
        scores = jnp.where(k_pos[None, :] <= q_pos[:, None], scores, -1e30)
        attn_prob = jax.nn.softmax(scores, axis=-1).astype(jnp.bfloat16)
        context = jnp.einsum("bkgst,btkh->bskgh", attn_prob, v_full, preferred_element_type=jnp.float32).astype(jnp.bfloat16)
        attn_out = jnp.einsum("bsn,nd->bsd", context.reshape(n_batch, seq_dev, -1), w_out, preferred_element_type=jnp.float32)
        hidden = jax.nn.gelu(jnp.einsum("bsd,df->bsf", h_mlp, w_up, preferred_element_type=jnp.float32), approximate=False).astype(jnp.bfloat16)
        mlp_out = jnp.einsum("bsf,fd->bsd", hidden, w_down, preferred_element_type=jnp.float32)
        y_out = (x_blk.astype(jnp.float32) + attn_out + mlp_out).astype(jnp.bfloat16)
        k_cache = lax.all_to_all(k_rot.transpose(0, 2, 1, 3), "sp", 1, 2, tiled=True)
        v_cache = lax.all_to_all(v_loc.transpose(0, 2, 1, 3), "sp", 1, 2, tiled=True)
        return y_out, k_cache, v_cache

    return jax.shard_map(local_layer, mesh=mesh, in_specs=(act_spec,) + (rep_spec,) * 8, out_specs=(act_spec, cache_spec, cache_spec), check_vma=False)
```

profile of v0, /device:TPU:27, one launch (start us, length us, event | category | flops | bytes accessed | tf_op | source)
XLA Modules:
  0.0 833.8 jit_solution(7400109865810602352)
XLA Ops:
  7.2 0.0 all-gather.4.cloned.1.call-start
  7.2 3.7 convert_reduce_fusion
  10.9 4.5 fusion.32
  15.5 0.0 copy-start.4
  15.5 0.0 copy-start.5
  15.5 32.0 %copy.23 = bf16[2048,16,3,128]{0,3,2,1:T(8,128)(2,1)} copy(bf16[2048,16,3,128]{3,1,2,0:T(8,128)(2,1)} %param.14) | data formatting | bytes 50331648 | tf_op args[5]
  47.5 0.0 copy-done.4
  47.5 0.0 copy-done.5
  47.5 47.3 %fusion.37 = bf16[12,128,16,3,128]{1,4,3,2,0:T(8,128)(2,1)} fusion(bf16[2048,16,3,128]{0,3,2,1:T(8,128)(2,1)} %copy.23, bf16[12,128,2048]{2,1,0:T(8,128)(2,1)} %param.9, f32[2048]{0:T(1024)S(1)} %copy-done.4, f32[2048]{0:T(1024)S(1)} %copy-done.5, f32[12,128]{1,0:T(8,128)S(1)} %add_rsqrt_fusion, f32[12,128]{1,0:T(8,128)S(1)} %broadcast_multiply_fusion), kind=kOutput, calls=%fused_computation.55 | convolution fusion | flops 38683017216 | bytes 50360320 | tf_op jit(solution)/shard_map/bsd,dkgh->bskgh/dot_general | solution.py:48
  94.8 22.5 %slice_bitcast_fusion.1 = (bf16[12,16,128,128]{2,3,1,0:T(8,128)(2,1)}, f32[12,128,16,1,128]{1,4,2,0,3:T(8,128)}, f32[12,128,16,1,128]{1,4,3,2,0:T(8,128)}, f32[1...) fusion(bf16[12,128,16,3,128]{1,4,3,2,0:T(8,128)(2,1)} %fusion.37), kind=kLoop, calls=%fused_computation.129 | loop fusion | flops 6291456 | bytes 69206016 | tf_op jit(solution)/shard_map/transpose | solution.py:64
  117.4 0.2 multiply_cosine_fusion
  117.6 0.0 copy-start
  117.6 0.0 copy-start.2
  117.6 5.6 subtract_convert_fusion
  123.2 6.1 fusion.106
  129.3 0.0 copy-done
  129.3 0.0 copy-done.2
  129.3 0.0 copy-start.6
  129.3 0.0 copy-start.7
  129.3 0.0 all-gather.4.cloned.1.call-update
  129.3 0.0 all-gather.6.cloned.1.call-start
  129.4 0.7 all-gather.6.cloned.1.call-update
  130.1 8.1 copy.32
  138.2 6.1 all-to-all-start
  144.3 8.0 copy.34
  152.3 0.0 copy-done.6
  152.3 0.0 copy-done.7
  152.4 75.7 %fusion.22 = (u16[128,8192]{1,0:T(8,128)(2,1)S(1)}, u16[128,8192]{1,0:T(8,128)(2,1)}, f32[12,128,8192]{2,1,0:T(8,128)}) fusion(bf16[2048,8192]{1,0:T(8,128)(2,1)} %param.16, bf16[12,128,2048]{2,1,0:T(8,128)(2,1)} %param.9, f32[2048]{0:T(1024)S(1)} %copy-done.6, f32[2048]{0:T(1024)S(1)} %copy-done.7, f32[12,128]{1,0:T(8,128)S(1)} %add_rsqrt_fusion, ...), kind=kOutput, calls=%fused_computation.38 | convolution fusion | flops 51719962624 | bytes 94400512 | tf_op jit(solution)/shard_map/bsd,df->bsf/dot_general | solution.py:60
  228.0 49.4 %all-to-all-done = bf16[12,16,128,128]{2,3,0,1:T(8,128)(2,1)} async-done(((bf16[12,16,128,128]{2,3,0,1:T(8,128)(2,1)}), bf16[12,16,128,128]{2,3,0,1:T(8,128)(2,1)}, u32[]{:S(2)}, u32[]{:S(2)}) %all-to-all-start) | async-done | bytes 6291488 | tf_op jit(solution)/shard_map/all_to_all | solution.py:63
  277.4 9.7 %all-to-all-start.1 = ((bf16[12,16,128,128]{2,3,0,1:T(8,128)(2,1)}), bf16[12,16,128,128]{2,3,0,1:T(8,128)(2,1)}, u32[]{:S(2)}, u32[]{:S(2)}) async-start(bf16[12,16,128,128]{2,3,0,1:T(8,128)(2,1)} %copy.34), calls=%async_computation.1 | async-start | bytes 12582912 | tf_op jit(solution)/shard_map/all_to_all | solution.py:64
  287.2 0.0 copy-start.1
  287.2 0.0 copy-start.3
  287.2 169.3 %fusion.15 = f32[12,128,2048]{2,1,0:T(8,128)} fusion(bf16[8192,2048]{1,0:T(8,128)(2,1)} %param.17, f32[12,128,8192]{2,1,0:T(8,128)} %get-tuple-element.16, u16[128,8192]{1,0:T(8,128)(2,1)} %get-tuple-element.4, u16[128,8192]{1,0:T(8,128)(2,1)S(1)} %get-tuple-element.3), kind=kOutput, calls=%fused_computation.31 | convolution fusion | flops 52420411392 | bytes 100663296 | tf_op jit(solution)/shard_map/bsf,fd->bsd/dot_general | solution.py:61
  456.5 0.1 iota_compare_fusion
  456.6 0.0 copy-done.1
  456.6 0.0 copy-done.3
  456.6 6.5 fusion.68
  463.1 8.2 fusion.69
  471.3 8.6 %copy.33 = bf16[12,2,8,128,128]{4,3,2,1,0:T(8,128)(2,1)} copy(bf16[12,2,8,128,128]{3,4,0,1,2:T(8,128)(2,1)} %bitcast.23) | data formatting | bytes 12582912 | tf_op jit(solution)/shard_map/all_to_all | solution.py:63
  479.9 0.0 all-to-all-done.1
  479.9 8.6 %copy.35 = bf16[12,2,8,128,128]{4,3,2,1,0:T(8,128)(2,1)} copy(bf16[12,2,8,128,128]{3,4,0,1,2:T(8,128)(2,1)} %bitcast.28) | data formatting | bytes 12582912 | tf_op jit(solution)/shard_map/all_to_all | solution.py:64
  488.5 17.6 %all-gather.4.cloned.1.call-done = bf16[12,1024,16,128]{1,3,2,0:T(8,128)(2,1)} async-done(((bf16[12,128,16,128]{1,3,2,0:T(8,128)(2,1)}), bf16[12,1024,16,128]{1,3,2,0:T(8,128)(2,1)}) %all-gather.4.cloned.1.call-update) | async-done | bytes 50331664 | tf_op jit(solution)/shard_map/all_gather | solution.py:53
  506.1 53.5 %fusion.1 = (f32[12,16,128]{2,1,0:T(8,128)S(1)}, f32[12,16,1024,128]{3,2,1,0:T(8,128)}) fusion(pred[128,1024]{0,1:T(8,128)(4,1)S(1)} %iota_compare_fusion, bf16[12,1024,16,128]{1,3,2,0:T(8,128)(2,1)} %all-gather.4.cloned.1.call-done, bf16[12,128,16,64]{1,3,2,0:T(8,128)(2,1)} %fusion.69, bf16[12,128,16,64]{1,3,2,0:T(8,128)(2,1)S(1)} %fusion.68), kind=kOutput, calls=%fused_computation.4 | convolution fusion | flops 6530506752 | bytes 157515776 | tf_op jit(solution)/shard_map/bskgh,btkh->bkgst/dot_general | solution.py:55
  559.6 31.2 %fusion = f32[12,16,128]{2,1,0:T(8,128)S(1)} fusion(f32[12,16,1024,128]{3,2,1,0:T(8,128)} %get-tuple-element.18, f32[12,16,128]{2,1,0:T(8,128)S(1)} %get-tuple-element.17, pred[128,1024]{0,1:T(8,128)(4,1)S(1)} %iota_compare_fusion), kind=kLoop, calls=%fused_computation.3 | loop fusion | flops 100638720 | bytes 100990976 | tf_op jit(solution)/shard_map/reduce_sum | solution.py:57
  590.8 160.0 %all-gather.6.cloned.1.call-done = bf16[12,1024,16,1,128]{1,4,3,2,0:T(8,128)(2,1)} async-done(((bf16[12,128,16,1,128]{1,4,3,2,0:T(8,128)(2,1)}), bf16[12,1024,16,1,128]{1,4,3,2,0:T(8,128)(2,1)}) %all-gather.6.cloned.1.call-update) | async-done | bytes 50331664 | tf_op jit(solution)/shard_map/all_gather | solution.py:54
  750.8 51.4 %fusion.63 = bf16[12,16,128,128]{3,2,1,0:T(8,128)(2,1)} fusion(f32[12,16,128]{2,1,0:T(8,128)S(1)} %fusion, f32[12,16,128]{2,1,0:T(8,128)S(1)} %get-tuple-element.17, f32[12,16,1024,128]{3,2,1,0:T(8,128)} %get-tuple-element.18, pred[128,1024]{0,1:T(8,128)(4,1)S(1)} %iota_compare_fusion, bf16[12,1024,16,1,128]{1,4,3,2,0:T(8,128)(2,1)} %all-gather.6.cloned.1.call-done), kind=kOutput, calls=%fused_computation.83 | convolution fusion | flops 6571425792 | bytes 157614080 | tf_op jit(solution)/shard_map/bkgst,btkh->bskgh/dot_general | solution.py:58
  802.2 24.6 %fusion.34 = bf16[12,128,2048]{2,1,0:T(8,128)(2,1)} fusion(f32[12,128,2048]{2,1,0:T(8,128)} %fusion.15, bf16[12,128,2048]{2,1,0:T(8,128)(2,1)} %param.9, bf16[12,128,2048]{1,2,0:T(8,128)(2,1)} %bitcast.114, bf16[2048,2048]{1,0:T(8,128)(2,1)} %param.15), kind=kOutput, calls=%fused_computation.52 | convolution fusion | flops 12897484800 | bytes 39845888 | tf_op jit(solution)/shard_map/bsn,nd->bsd/dot_general | solution.py:59
  (5 shorter events, 0.0 us)
Async XLA Ops:
  7.2 498.9 %all-gather.4.cloned.1.call-start = ((), (), s32[]{:S(2)}) async-start(), calls=%async_computation.2 | async-start | bytes 56623104 | tf_op jit(solution)/shard_map/all_gather | solution.py:53
  15.5 32.0 %copy-start.4 = (f32[2048]{0:T(1024)S(1)}, f32[2048]{0:T(1024)}, u32[]{:S(2)}) copy-start(f32[2048]{0:T(1024)} %param.11) | copy-start | bytes 24580
  15.5 32.0 %copy-start.5 = (f32[2048]{0:T(1024)S(1)}, f32[2048]{0:T(1024)}, u32[]{:S(2)}) copy-start(f32[2048]{0:T(1024)} %param.10) | copy-start | bytes 24580
  117.6 11.7 %copy-start = (f32[128,64]{0,1:T(8,128)}, f32[128,64]{0,1:T(8,128)S(1)}, u32[]{:S(2)}) copy-start(f32[128,64]{0,1:T(8,128)S(1)} %get-tuple-element.14) | copy-start | bytes 98308
  117.6 11.7 %copy-start.2 = (f32[128,64]{0,1:T(8,128)}, f32[128,64]{0,1:T(8,128)S(1)}, u32[]{:S(2)}) copy-start(f32[128,64]{0,1:T(8,128)S(1)} %get-tuple-element.15) | copy-start | bytes 98308
  129.3 23.0 %copy-start.6 = (f32[2048]{0:T(1024)S(1)}, f32[2048]{0:T(1024)}, u32[]{:S(2)}) copy-start(f32[2048]{0:T(1024)} %param.13) | copy-start | bytes 24580
  129.3 23.0 %copy-start.7 = (f32[2048]{0:T(1024)S(1)}, f32[2048]{0:T(1024)}, u32[]{:S(2)}) copy-start(f32[2048]{0:T(1024)} %param.12) | copy-start | bytes 24580
  129.3 621.5 %all-gather.6.cloned.1.call-start = ((), (), s32[]{:S(2)}) async-start(), calls=%async_computation.3 | async-start | bytes 56623104 | tf_op jit(solution)/shard_map/all_gather | solution.py:54
  138.2 139.2 %all-to-all-start = ((bf16[12,16,128,128]{2,3,0,1:T(8,128)(2,1)}), bf16[12,16,128,128]{2,3,0,1:T(8,128)(2,1)}, u32[]{:S(2)}, u32[]{:S(2)}) async-start(bf16[12,16,128,128]{2,3,0,1:T(8,128)(2,1)} %copy.32), calls=%async_computation | async-start | bytes 12582912 | tf_op jit(solution)/shard_map/all_to_all | solution.py:63
  277.4 202.5 %all-to-all-start.1 = ((bf16[12,16,128,128]{2,3,0,1:T(8,128)(2,1)}), bf16[12,16,128,128]{2,3,0,1:T(8,128)(2,1)}, u32[]{:S(2)}, u32[]{:S(2)}) async-start(bf16[12,16,128,128]{2,3,0,1:T(8,128)(2,1)} %copy.34), calls=%async_computation.1 | async-start | bytes 12582912 | tf_op jit(solution)/shard_map/all_to_all | solution.py:64
  287.2 169.4 %copy-start.1 = (f32[128,64]{0,1:T(8,128)S(1)}, f32[128,64]{0,1:T(8,128)}, u32[]{:S(2)}) copy-start(f32[128,64]{0,1:T(8,128)} %copy-done) | copy-start | bytes 98308
  287.2 169.4 %copy-start.3 = (f32[128,64]{0,1:T(8,128)S(1)}, f32[128,64]{0,1:T(8,128)}, u32[]{:S(2)}) copy-start(f32[128,64]{0,1:T(8,128)} %copy-done.2) | copy-start | bytes 98308
Sparse Core Ops, SparseCore 0:
  129.5 376.5 all-gather.3
  508.6 242.2 all-gather.5
where the time goes:
time: 840 us; the launch traced here: 834 us
  matrix products  422 us (50%)
  waiting for transfers between devices  228 us (27%)
  other arithmetic  88.6 us (11%)
  local copies, waits for them, and re-layouts  65.4 us (8%)
  starting transfers between devices  15.9 us (2%)
  between operations  14.4 us (2%)
    dot_general x1, matrix products, local_layer(): jnp.einsum('bsf,fd->bsd', hidden, w_down, preferred_element_type=jnp.floa...  169 us
    all_gather x1, waiting for transfers between devices, local_layer(): v_full = lax.all_gather(v_loc, 'sp', axis=1, tiled=True)  160 us
    dot_general x1, matrix products, local_layer(): jnp.einsum('bsd,df->bsf', h_mlp, w_up, preferred_element_type=jnp.float32)  75.7 us
    dot_general x1, matrix products, local_layer(): jnp.einsum('bskgh,btkh->bkgst', q_rot, k_full, preferred_element_type=jnp...  53.5 us
    dot_general x1, matrix products, local_layer(): jnp.einsum('bkgst,btkh->bskgh', attn_prob, v_full, preferred_element_type...  51.4 us
    all_to_all x1, waiting for transfers between devices, local_layer(): lax.all_to_all(k_rot.transpose(0, 2, 1, 3), 'sp', 1, 2, tiled=True)  49.4 us
    dot_general x1, matrix products, local_layer(): jnp.einsum('bsd,dkgh->bskgh', h_attn, w_qkv, preferred_element_type=jnp.f...  47.3 us
    unnamed x17, local copies, waits for them, and re-layouts  32 us
  transfers between devices with their start and end apart: 4, of which 3 were waited for; matrix products, arithmetic and copies ran while one was open for 45% of the time, Pallas kernels for 0%

commit v1 on v0

v1 whole, which is shorter than its diff:
```python
import functools

import jax
import jax.numpy as jnp
from jax import lax
from jax.experimental import pallas as pl
from jax.experimental.pallas import tpu as pltpu
from jax.sharding import PartitionSpec as P

LN_EPS = 1e-5
ROPE_BASE = 10000.0
LOG2E = 1.4426950408889634
N_CHUNKS = 4
UP_TILE = 512
QKV_TILE = 1024
Q_TILE = 256
F32 = jnp.float32
BF16 = jnp.bfloat16


def rope_tables(positions, head_dim):
    half_dim = head_dim // 2
    inv_freq = ROPE_BASE ** (-2.0 * jnp.arange(half_dim, dtype=F32) / head_dim)
    angles = positions.astype(F32)[:, None] * inv_freq[None, :]
    cos_t, sin_t = jnp.cos(angles), jnp.sin(angles)
    return jnp.concatenate([cos_t, cos_t], -1), jnp.concatenate([-sin_t, sin_t], -1)


def causal_head(q, k, v, write):
    seq, head_dim = q.shape
    scale = LOG2E * head_dim**-0.5
    rows = lax.broadcasted_iota(jnp.int32, (Q_TILE, Q_TILE), 0)
    cols = lax.broadcasted_iota(jnp.int32, (Q_TILE, Q_TILE), 1)
    for i in range(seq // Q_TILE):
        lo, hi = i * Q_TILE, (i + 1) * Q_TILE
        q_i = q[lo:hi]
        dims = (((1,), (1,)), ((), ()))
        diag = lax.dot_general(q_i, k[lo:hi], dims, preferred_element_type=F32)
        diag = jnp.where(cols <= rows, diag, -1e30)
        top = jnp.max(diag, axis=-1, keepdims=True)
        if lo:
            past = lax.dot_general(q_i, k[:lo], dims, preferred_element_type=F32)
            top = jnp.maximum(top, jnp.max(past, axis=-1, keepdims=True))
        diag = jnp.exp2((diag - top) * scale)
        total = jnp.sum(diag, axis=-1, keepdims=True)
        if lo:
            past = jnp.exp2((past - top) * scale)
            total = total + jnp.sum(past, axis=-1, keepdims=True)
        inv = 1.0 / total
        out = jnp.dot((diag * inv).astype(BF16), v[lo:hi], preferred_element_type=F32)
        if lo:
            out = out + jnp.dot((past * inv).astype(BF16), v[:lo], preferred_element_type=F32)
        write(i, out.astype(BF16))


def layer_kernel(
    n,
    x_hbm,
    cos_ref,
    sin_ref,
    ln_aw,
    ln_ab,
    ln_mw,
    ln_mb,
    w_qkv,
    w_up,
    w_down,
    resid_hbm,
    recv,
    ctx_recv,
    send,
    ctx_send,
    x_buf,
    h_attn,
    h_mlp,
    acc,
    qkv_acc,
    own,
    own_ctx,
    x_sem,
    own_sem,
    out_sem,
    send_sem,
    recv_sem,
    ctx_send_sem,
    ctx_recv_sem,
):
    me = lax.axis_index("sp")
    n_batch, _, heads, seq_dev, head_dim = send.shape[1:]
    width = x_hbm.shape[1]
    nb = n_batch // N_CHUNKS
    rows = nb * seq_dev
    ffn = w_up.shape[1]
    dests = QKV_TILE // (heads * head_dim)

    def peer(step):
        return lax.bitwise_xor(me, step)

    def put(chunk, to, frm):
        bs = pl.ds(chunk * nb, nb)
        return pltpu.make_async_remote_copy(
            src_ref=send.at[:, bs, to],
            dst_ref=recv.at[:, bs, :, frm],
            send_sem=send_sem.at[chunk, to],
            recv_sem=recv_sem.at[chunk, frm],
            device_id={"sp": to},
            device_id_type=pl.DeviceIdType.MESH,
        )

    def put_ctx(chunk, to, frm):
        bs = pl.ds(chunk * nb, nb)
        return pltpu.make_async_remote_copy(
            src_ref=ctx_send.at[bs, to],
            dst_ref=ctx_recv.at[bs, frm],
            send_sem=ctx_send_sem.at[chunk, to],
            recv_sem=ctx_recv_sem.at[chunk, frm],
            device_id={"sp": to},
            device_id_type=pl.DeviceIdType.MESH,
        )

    def put_own(chunk):
        return pltpu.make_async_copy(own, recv.at[:, pl.ds(chunk * nb, nb), :, me], own_sem.at[0])

    def put_own_ctx(chunk):
        return pltpu.make_async_copy(own_ctx, ctx_recv.at[pl.ds(chunk * nb, nb), me], own_sem.at[1])

    def get_x(chunk):
        return pltpu.make_async_copy(x_hbm.at[pl.ds(chunk * rows, rows)], x_buf, x_sem)

    get_x(0).start()
    barrier = pltpu.get_barrier_semaphore()
    for step in range(1, n):
        pl.semaphore_signal(barrier, inc=1, device_id={"sp": peer(step)}, device_id_type=pl.DeviceIdType.MESH)
    pl.semaphore_wait(barrier, n - 1)

    @pl.loop(0, N_CHUNKS)
    def _(chunk):
        get_x(chunk).wait()

        @pl.loop(0, rows // 16)
        def _(i):
            r = pl.ds(pl.multiple_of(i * 16, 16), 16)
            g = pl.ds(pl.multiple_of(chunk * rows + i * 16, 16), 16)
            xf = x_buf[r, :].astype(F32)
            mean = jnp.sum(xf, axis=-1, keepdims=True) * (1.0 / width)
            dev = xf - mean
            var = jnp.sum(dev * dev, axis=-1, keepdims=True) * (1.0 / width)
            unit = dev * lax.rsqrt(var + LN_EPS)
            h_attn[r, :] = (unit * ln_aw[...] + ln_ab[...]).astype(BF16)
            h_mlp[g, :] = (unit * ln_mw[...] + ln_mb[...]).astype(BF16)
            acc[g, :] = xf

        @pl.when(chunk + 1 < N_CHUNKS)
        def _():
            get_x(chunk + 1).start()

        @pl.when(chunk > 0)
        def _():
            put_own(chunk - 1).wait()

        def qkv_body(w_ref, o_ref):
            kind, part = pl.program_id(0), pl.program_id(1)
            qkv_acc[...] = jnp.dot(h_attn[...], w_ref[...], preferred_element_type=F32)

            @pl.when(kind < 2)
            def _():
                for d in range(dests * heads):
                    for b in range(nb):
                        u = qkv_acc[b * seq_dev : (b + 1) * seq_dev, d * head_dim : (d + 1) * head_dim]
                        u = u.astype(BF16).astype(F32)
                        u = u * cos_ref[...] + pltpu.roll(u, head_dim // 2, 1) * sin_ref[...]
                        o_ref[0, b, d // heads, d % heads] = u.astype(BF16)

            @pl.when(kind == 2)
            def _():
                for d in range(dests * heads):
                    for b in range(nb):
                        u = qkv_acc[b * seq_dev : (b + 1) * seq_dev, d * head_dim : (d + 1) * head_dim]
                        o_ref[0, b, d // heads, d % heads] = u.astype(BF16)

            @pl.when(me // dests == part)
            def _():
                own[kind] = o_ref[0, :, lax.rem(me, dests)]

        parts = n // dests
        pltpu.emit_pipeline(
            qkv_body,
            grid=(3, parts),
            in_specs=[pl.BlockSpec((width, QKV_TILE), lambda t, p: (0, t * parts + p))],
            out_specs=[
                pl.BlockSpec((1, nb, dests, heads, seq_dev, head_dim), lambda t, p: (t, chunk, p, 0, 0, 0))
            ],
        )(w_qkv, send)
        for step in range(1, n):
            put(chunk, peer(step), me).start()
        put_own(chunk).start()

    @pl.loop(0, N_CHUNKS)
    def _(chunk):
        def mlp_body(up_ref, down_ref):
            blocks = n_batch * seq_dev // 512
            for r in range(blocks):
                rs = pl.ds(r * 512, 512)
                up = jnp.dot(h_mlp[rs, :], up_ref[...], preferred_element_type=F32)
                hid = (0.5 * up * (1.0 + lax.erf(up * 0.5**0.5))).astype(BF16)
                acc[rs, :] += jnp.dot(hid, down_ref[...], preferred_element_type=F32)

        steps = ffn // UP_TILE // N_CHUNKS
        pltpu.emit_pipeline(
            mlp_body,
            grid=(steps,),
            in_specs=[
                pl.BlockSpec((width, UP_TILE), lambda f: (0, chunk * steps + f)),
                pl.BlockSpec((UP_TILE, width), lambda f: (chunk * steps + f, 0)),
            ],
        )(w_up, w_down)

        @pl.when(chunk == N_CHUNKS - 1)
        def _():
            pltpu.make_async_copy(acc, resid_hbm, out_sem).start()

        @pl.when(chunk == 0)
        def _():
            put_own(N_CHUNKS - 1).wait()

        for step in range(1, n):
            put(chunk, me, peer(step)).wait_recv()

        @pl.when(chunk > 0)
        def _():
            put_own_ctx(chunk - 1).wait()

        def attn_body(q_ref, k_ref, v_ref, o_ref):
            b, h = pl.program_id(0), pl.program_id(1)
            flat = lambda ref: ref[...].reshape(n * seq_dev, head_dim)
            per = Q_TILE // seq_dev

            def write(i, out):
                o_ref[0, i * per : (i + 1) * per, 0] = out.reshape(per, seq_dev, head_dim)

            causal_head(flat(q_ref), flat(k_ref), flat(v_ref), write)
            own_ctx[b, h] = o_ref[0, me, 0]

        spec = lambda t: pl.BlockSpec(
            (1, 1, 1, n, seq_dev, head_dim), lambda b, h: (t, chunk * nb + b, h, 0, 0, 0)
        )
        pltpu.emit_pipeline(
            attn_body,
            grid=(nb, heads),
            in_specs=[spec(0), spec(1), spec(2)],
            out_specs=[
                pl.BlockSpec((1, n, 1, seq_dev, head_dim), lambda b, h: (chunk * nb + b, 0, h, 0, 0))
            ],
        )(recv, recv, recv, ctx_send)
        for step in range(1, n):
            put_ctx(chunk, peer(step), me).start()
        put_own_ctx(chunk).start()

    put_own_ctx(N_CHUNKS - 1).wait()
    pltpu.make_async_copy(acc, resid_hbm, out_sem).wait()

    @pl.loop(0, N_CHUNKS)
    def _(chunk):
        for step in range(1, n):
            put(chunk, peer(step), me).wait_send()
            put_ctx(chunk, peer(step), me).wait_send()
            put_ctx(chunk, me, peer(step)).wait_recv()


def out_kernel(ctx_ref, w_ref, resid_ref, k_in, v_in, y_ref, k_out, v_out, rows_ref):
    nb, n, heads, seq_dev, head_dim = ctx_ref.shape
    for b in range(nb):
        for s in range(n):
            for h in range(heads):
                col = (s * heads + h) * head_dim
                rows_ref[b * seq_dev : (b + 1) * seq_dev, col : col + head_dim] = ctx_ref[b, s, h]
    attn = jnp.dot(rows_ref[...], w_ref[...], preferred_element_type=F32)
    y_ref[...] = (resid_ref[...] + attn).astype(BF16)
    k_out[...] = k_in[0]
    v_out[...] = v_in[0]


def solution(mesh):
    n = mesh.shape["sp"]

    def local_layer(x_blk, ln_attn_w, ln_attn_b, ln_mlp_w, ln_mlp_b, w_qkv, w_out, w_up, w_down):
        n_batch, seq_dev, width = x_blk.shape
        groups, head_dim = w_qkv.shape[1], w_qkv.shape[3]
        heads = groups // n
        nb = n_batch // N_CHUNKS
        rows = n_batch * seq_dev
        ffn = w_up.shape[1]
        q_pos = lax.axis_index("sp") * seq_dev + jnp.arange(seq_dev)
        cos_t, sin_t = rope_tables(q_pos, head_dim)
        w_cols = w_qkv.transpose(0, 2, 1, 3).reshape(width, -1)
        row = lambda p: p.reshape(1, width)
        anywhere = pl.BlockSpec(memory_space=pl.ANY)
        vmem = pl.BlockSpec(memory_space=pltpu.VMEM)
        flops = 2 * rows * width * (3 * width + 2 * ffn) + 2 * rows * n * seq_dev * width * 2
        resid, recv, ctx_recv, _, _ = pl.pallas_call(
            functools.partial(layer_kernel, n),
            out_shape=[
                jax.ShapeDtypeStruct((rows, width), F32),
                jax.ShapeDtypeStruct((3, n_batch, heads, n, seq_dev, head_dim), BF16),
                jax.ShapeDtypeStruct((n_batch, n, heads, seq_dev, head_dim), BF16),
                jax.ShapeDtypeStruct((3, n_batch, n, heads, seq_dev, head_dim), BF16),
                jax.ShapeDtypeStruct((n_batch, n, heads, seq_dev, head_dim), BF16),
            ],
            in_specs=[anywhere] + [vmem] * 6 + [anywhere] * 3,
            out_specs=[anywhere] * 5,
            scratch_shapes=[
                pltpu.VMEM((nb * seq_dev, width), BF16),
                pltpu.VMEM((nb * seq_dev, width), BF16),
                pltpu.VMEM((rows, width), BF16),
                pltpu.VMEM((rows, width), F32),
                pltpu.VMEM((nb * seq_dev, QKV_TILE), F32),
                pltpu.VMEM((3, nb, heads, seq_dev, head_dim), BF16),
                pltpu.VMEM((nb, heads, seq_dev, head_dim), BF16),
                pltpu.SemaphoreType.DMA,
                pltpu.SemaphoreType.DMA((2,)),
                pltpu.SemaphoreType.DMA,
                pltpu.SemaphoreType.DMA((N_CHUNKS, n)),
                pltpu.SemaphoreType.DMA((N_CHUNKS, n)),
                pltpu.SemaphoreType.DMA((N_CHUNKS, n)),
                pltpu.SemaphoreType.DMA((N_CHUNKS, n)),
            ],
            compiler_params=pltpu.CompilerParams(
                collective_id=0, has_side_effects=True, vmem_limit_bytes=60 * 2**20
            ),
            cost_estimate=pl.CostEstimate(flops=flops, bytes_accessed=3 * 10**8, transcendentals=10**7),
            name="layer",
        )(
            x_blk.reshape(rows, width),
            cos_t,
            sin_t,
            row(ln_attn_w),
            row(ln_attn_b),
            row(ln_mlp_w),
            row(ln_mlp_b),
            w_cols,
            w_up,
            w_down,
        )
        cache = jax.ShapeDtypeStruct((n_batch, heads, n, seq_dev, head_dim), BF16)
        block = nb * seq_dev
        cache_block = (nb, heads, n, seq_dev, head_dim)
        y_out, k_cache, v_cache = pl.pallas_call(
            out_kernel,
            grid=(N_CHUNKS,),
            out_shape=[jax.ShapeDtypeStruct((rows, width), BF16), cache, cache],
            in_specs=[
                pl.BlockSpec((nb, n, heads, seq_dev, head_dim), lambda i: (i, 0, 0, 0, 0)),
                pl.BlockSpec((width, width), lambda i: (0, 0)),
                pl.BlockSpec((block, width), lambda i: (i, 0)),
                pl.BlockSpec((1, *cache_block), lambda i: (1, i, 0, 0, 0, 0)),
                pl.BlockSpec((1, *cache_block), lambda i: (2, i, 0, 0, 0, 0)),
            ],
            out_specs=[
                pl.BlockSpec((block, width), lambda i: (i, 0)),
                pl.BlockSpec(cache_block, lambda i: (i, 0, 0, 0, 0)),
                pl.BlockSpec(cache_block, lambda i: (i, 0, 0, 0, 0)),
            ],
            scratch_shapes=[pltpu.VMEM((block, width), BF16)],
            compiler_params=pltpu.CompilerParams(vmem_limit_bytes=60 * 2**20),
            cost_estimate=pl.CostEstimate(
                flops=2 * rows * width * width, bytes_accessed=6 * 10**7, transcendentals=0
            ),
            name="out",
        )(ctx_recv, w_out, resid, recv, recv)
        shape = (n_batch, heads, n * seq_dev, head_dim)
        return y_out.reshape(x_blk.shape), k_cache.reshape(shape), v_cache.reshape(shape)

    act_spec, cache_spec = P("dp", "sp", None), P("dp", "sp", None, None)
    return jax.shard_map(
        local_layer,
        mesh=mesh,
        in_specs=(act_spec,) + (P(),) * 8,
        out_specs=(act_spec, cache_spec, cache_spec),
        check_vma=False,
    )
```

time: 840 us -> 355 us (0.42)
  matrix products: 422 us -> 0 us
  Pallas kernels: 0 us -> 325 us
  waiting for transfers between devices: 228 us -> 0 us
  other arithmetic: 88.6 us -> 1.08 us
  local copies, waits for them, and re-layouts: 65.4 us -> 25.6 us
  starting transfers between devices: 15.9 us -> 0 us
  between operations: 14.4 us -> 0.66 us
    dot_general x6 -> x0, matrix products: 422 us -> none  [the longest x1 169 us: local_layer(): jnp.einsum('bsf,fd->bsd', hidden, w_down, preferred_element_type=jnp.floa...]
    pallas_call x0 -> x2, Pallas kernels: none -> 325 us  [the longest x1 299 us: local_layer(): pl.pallas_call(functools.partial(layer_kernel, n), out_shape=[jax.ShapeDt...]
    all_gather x2 -> x0, waiting for transfers between devices: 178 us -> none  [the longest x1 160 us: local_layer(): v_full = lax.all_gather(v_loc, 'sp', axis=1, tiled=True)]
    all_to_all x2 -> x0, waiting for transfers between devices: 49.4 us -> none  [the longest x1 49.4 us: local_layer(): lax.all_to_all(k_rot.transpose(0, 2, 1, 3), 'sp', 1, 2, tiled=True)]
    reduce_sum x3 -> x0, other arithmetic: 39.4 us -> none  [the longest x1 31.2 us: local_layer(): attn_prob = jax.nn.softmax(scores, axis=-1).astype(jnp.bfloat16)]
    transpose x2 -> x0, other arithmetic: 28.6 us -> none  [the longest x1 22.5 us: local_layer(): v_loc.transpose(0, 2, 1, 3)]
    all_to_all x2 -> x0, local copies, waits for them, and re-layouts: 17.3 us -> none  [the longest x1 8.63 us: local_layer(): lax.all_to_all(v_loc.transpose(0, 2, 1, 3), 'sp', 1, 2, tiled=True)]
    transpose x2 -> x0, local copies, waits for them, and re-layouts: 16.2 us -> none  [the longest x1 8.11 us: local_layer(): k_rot.transpose(0, 2, 1, 3)]
  transfers between devices with their start and end apart: 4 -> 0, of which waited for: 3 -> 0; matrix products, arithmetic and copies ran while one was open for 45% -> 0% of each run, Pallas kernels for 0% -> 0%
where the time goes in v1:
time: 355 us; the launch traced here: 353 us
  Pallas kernels  325 us (92%)
  local copies, waits for them, and re-layouts  25.6 us (7%)
    pallas_call x1, Pallas kernels, local_layer(): pl.pallas_call(functools.partial(layer_kernel, n), out_shape=[jax.ShapeDt...  299 us
    pallas_call x1, Pallas kernels, local_layer(): pl.pallas_call(out_kernel, grid=(N_CHUNKS,), out_shape=[jax.ShapeDtypeStr...  26.3 us
    unnamed x1, local copies, waits for them, and re-layouts  25.6 us

profile of v1, /device:TPU:27, one launch (start us, length us, event | category | flops | bytes accessed | tf_op | source)
XLA Modules:
  0.0 352.7 jit_solution(9550689528548097614)
XLA Ops:
  0.7 0.3 fusion
  1.0 0.8 pad_maximum_fusion
  1.7 25.6 %copy.14 = bf16[256,8,48,128]{3,1,2,0:T(8,128)(2,1)} copy(bf16[256,8,48,128]{3,2,1,0:T(8,128)(2,1)} %bitcast.14) | data formatting | bytes 50331648
  27.4 299.1 %layer.1 = (f32[1536,2048]{1,0:T(8,128)}, bf16[3,12,2,8,128,128]{5,4,3,2,1,0:T(8,128)(2,1)}, bf16[12,8,2,128,128]{4,3,2,1,0:T(8,128)(2,1)}, bf16[3,12,8,2,128,12...) custom-call(bf16[1536,2048]{1,0:T(8,128)(2,1)} %bitcast.16, f32[128,128]{1,0:T(8,128)} %get-tuple-element.18.cos_ref, ...), custom_call_target="tpu_custom_call" | custom-call | flops 154618822656 | bytes 300000000 | tf_op jit(solution)/shard_map/layer/pallas_call | solution.py:300
  326.5 26.3 %out.1 = (bf16[1536,2048]{1,0:T(8,128)(2,1)}, bf16[12,2,8,128,128]{4,3,2,1,0:T(8,128)(2,1)}, bf16[12,2,8,128,128]{4,3,2,1,0:T(8,128)(2,1)}) custom-call(bf16[12,8,2,128,128]{4,3,2,1,0:T(8,128)(2,1)} %get-tuple-element.9.ctx_ref, bf16[2048,2048]{1,0:T(8,128)(2,1)} %w_ref.1, f32[1536,2048]{1,0:T(8,128)} %get-tuple-element.10.resid_ref, ...), custom_call_target="tpu_custom_call" | custom-call | flops 12884901888 | bytes 60000000 | tf_op jit(solution)/shard_map/out/pallas_call | solution.py:347
  (2 shorter events, 0.0 us)

commit v2 on v1

--- a/solution.py
+++ b/solution.py
@@ -12,7 +12,7 @@
 LOG2E = 1.4426950408889634
 N_CHUNKS = 4
 UP_TILE = 512
-QKV_TILE = 1024
+QKV_HEADS = 8
 Q_TILE = 256
 F32 = jnp.float32
 BF16 = jnp.bfloat16
@@ -70,14 +70,12 @@
     ctx_recv,
     send,
     ctx_send,
-    x_buf,
-    h_attn,
     h_mlp,
     acc,
-    qkv_acc,
-    own,
     own_ctx,
     x_sem,
+    w_sem,
+    bounce_sem,
     own_sem,
     out_sem,
     send_sem,
@@ -91,18 +89,20 @@
     nb = n_batch // N_CHUNKS
     rows = nb * seq_dev
     ffn = w_up.shape[1]
-    dests = QKV_TILE // (heads * head_dim)
+    dests = QKV_HEADS // heads
+    parts = n // dests
+    blocks = 3 * parts
 
     def peer(step):
         return lax.bitwise_xor(me, step)
 
-    def put(chunk, to, frm):
+    def put(chunk, kind, to, frm):
         bs = pl.ds(chunk * nb, nb)
         return pltpu.make_async_remote_copy(
-            src_ref=send.at[:, bs, to],
-            dst_ref=recv.at[:, bs, :, frm],
-            send_sem=send_sem.at[chunk, to],
-            recv_sem=recv_sem.at[chunk, frm],
+            src_ref=send.at[kind, bs, to],
+            dst_ref=recv.at[kind, bs, :, frm],
+            send_sem=send_sem.at[chunk, kind, to],
+            recv_sem=recv_sem.at[chunk, kind, frm],
             device_id={"sp": to},
             device_id_type=pl.DeviceIdType.MESH,
         )
@@ -118,82 +118,142 @@
             device_id_type=pl.DeviceIdType.MESH,
         )
 
-    def put_own(chunk):
-        return pltpu.make_async_copy(own, recv.at[:, pl.ds(chunk * nb, nb), :, me], own_sem.at[0])
-
     def put_own_ctx(chunk):
-        return pltpu.make_async_copy(own_ctx, ctx_recv.at[pl.ds(chunk * nb, nb), me], own_sem.at[1])
-
-    def get_x(chunk):
-        return pltpu.make_async_copy(x_hbm.at[pl.ds(chunk * rows, rows)], x_buf, x_sem)
-
-    get_x(0).start()
-    barrier = pltpu.get_barrier_semaphore()
-    for step in range(1, n):
-        pl.semaphore_signal(barrier, inc=1, device_id={"sp": peer(step)}, device_id_type=pl.DeviceIdType.MESH)
-    pl.semaphore_wait(barrier, n - 1)
-
-    @pl.loop(0, N_CHUNKS)
-    def _(chunk):
-        get_x(chunk).wait()
-
-        @pl.loop(0, rows // 16)
-        def _(i):
-            r = pl.ds(pl.multiple_of(i * 16, 16), 16)
-            g = pl.ds(pl.multiple_of(chunk * rows + i * 16, 16), 16)
-            xf = x_buf[r, :].astype(F32)
-            mean = jnp.sum(xf, axis=-1, keepdims=True) * (1.0 / width)
-            dev = xf - mean
-            var = jnp.sum(dev * dev, axis=-1, keepdims=True) * (1.0 / width)
-            unit = dev * lax.rsqrt(var + LN_EPS)
-            h_attn[r, :] = (unit * ln_aw[...] + ln_ab[...]).astype(BF16)
-            h_mlp[g, :] = (unit * ln_mw[...] + ln_mb[...]).astype(BF16)
-            acc[g, :] = xf
-
-        @pl.when(chunk + 1 < N_CHUNKS)
-        def _():
-            get_x(chunk + 1).start()
-
-        @pl.when(chunk > 0)
-        def _():
-            put_own(chunk - 1).wait()
-
-        def qkv_body(w_ref, o_ref):
-            kind, part = pl.program_id(0), pl.program_id(1)
-            qkv_acc[...] = jnp.dot(h_attn[...], w_ref[...], preferred_element_type=F32)
+        return pltpu.make_async_copy(own_ctx, ctx_recv.at[pl.ds(chunk * nb, nb), me], own_sem.at[3])
+
+    def qkv_phase(x_buf, h_attn, w_nat, w_cols, qkv_acc, out_buf, own):
+        def get_x(chunk):
+            return pltpu.make_async_copy(x_hbm.at[pl.ds(chunk * rows, rows)], x_buf, x_sem)
+
+        def get_w(block):
+            slot = lax.rem(block, 2)
+            src = w_qkv.at[:, block // parts, pl.ds(lax.rem(block, parts) * QKV_HEADS, QKV_HEADS)]
+            return pltpu.make_async_copy(src, w_nat.at[slot], w_sem.at[slot])
+
+        def bounce(step):
+            slot, block = lax.rem(step, 2), lax.rem(step, blocks)
+            dst = send.at[
+                block // parts, pl.ds(step // blocks * nb, nb), pl.ds(lax.rem(block, parts) * dests, dests)
+            ]
+            return pltpu.make_async_copy(out_buf.at[slot], dst, bounce_sem.at[slot])
+
+        def put_own(chunk, kind):
+            dst = recv.at[kind, pl.ds(chunk * nb, nb), :, me]
+            return pltpu.make_async_copy(own.at[kind], dst, own_sem.at[kind])
+
+        def send_block(step):
+            bounce(step).wait()
+            block = lax.rem(step, blocks)
+            for d in range(dests):
+                to = lax.rem(block, parts) * dests + lax.rem(me + d, dests)
+
+                @pl.when(to != me)
+                def _():
+                    put(step // blocks, block // parts, to, me).start()
+
+        get_x(0).start()
+        get_w(0).start()
+        barrier = pltpu.get_barrier_semaphore()
+        for step in range(1, n):
+            pl.semaphore_signal(
+                barrier, inc=1, device_id={"sp": peer(step)}, device_id_type=pl.DeviceIdType.MESH
+            )
+
+        @pl.loop(0, N_CHUNKS * blocks)
+        def _(step):
+            chunk, block = step // blocks, lax.rem(step, blocks)
+            kind, part = block // parts, lax.rem(block, parts)
+            slot = lax.rem(step, 2)
+
+            @pl.when(block == 0)
+            def _():
+                get_x(chunk).wait()
+
+                @pl.loop(0, rows // 16)
+                def _(i):
+                    r = pl.ds(pl.multiple_of(i * 16, 16), 16)
+                    g = pl.ds(pl.multiple_of(chunk * rows + i * 16, 16), 16)
+                    xf = x_buf[r, :].astype(F32)
+                    mean = jnp.sum(xf, axis=-1, keepdims=True) * (1.0 / width)
+                    dev = xf - mean
+                    var = jnp.sum(dev * dev, axis=-1, keepdims=True) * (1.0 / width)
+                    unit = dev * lax.rsqrt(var + LN_EPS)
+                    h_attn[r, :] = (unit * ln_aw[...] + ln_ab[...]).astype(BF16)
+                    h_mlp[g, :] = (unit * ln_mw[...] + ln_mb[...]).astype(BF16)
+                    acc[g, :] = xf
+
+                @pl.when(chunk + 1 < N_CHUNKS)
+                def _():
+                    get_x(chunk + 1).start()
+
+            @pl.when(chunk == 0)
+            def _():
+                get_w(block).wait()
+
+                @pl.when(block + 1 < blocks)
+                def _():
+                    get_w(block + 1).start()
+
+                @pl.loop(0, width // 128)
+                def _(i):
+                    r = pl.ds(pl.multiple_of(i * 128, 128), 128)
+                    by_head = jnp.swapaxes(w_nat[slot, r].astype(F32), 0, 1)
+                    for h in range(QKV_HEADS):
+                        w_cols[block, r, h * head_dim : (h + 1) * head_dim] = by_head[h].astype(BF16)
+
+            qkv_acc[...] = jnp.dot(h_attn[...], w_cols[block], preferred_element_type=F32)
+
+            def take(b, h):
+                u = qkv_acc[b * seq_dev : (b + 1) * seq_dev, h * head_dim : (h + 1) * head_dim]
+                return u.astype(BF16)
 
             @pl.when(kind < 2)
             def _():
-                for d in range(dests * heads):
+                for h in range(QKV_HEADS):
                     for b in range(nb):
-                        u = qkv_acc[b * seq_dev : (b + 1) * seq_dev, d * head_dim : (d + 1) * head_dim]
-                        u = u.astype(BF16).astype(F32)
+                        u = take(b, h).astype(F32)
                         u = u * cos_ref[...] + pltpu.roll(u, head_dim // 2, 1) * sin_ref[...]
-                        o_ref[0, b, d // heads, d % heads] = u.astype(BF16)
+                        out_buf[slot, b, h // heads, h % heads] = u.astype(BF16)
 
             @pl.when(kind == 2)
             def _():
-                for d in range(dests * heads):
+                for h in range(QKV_HEADS):
                     for b in range(nb):
-                        u = qkv_acc[b * seq_dev : (b + 1) * seq_dev, d * head_dim : (d + 1) * head_dim]
-                        o_ref[0, b, d // heads, d % heads] = u.astype(BF16)
+                        out_buf[slot, b, h // heads, h % heads] = take(b, h)
+
+            bounce(step).start()
 
             @pl.when(me // dests == part)
             def _():
-                own[kind] = o_ref[0, :, lax.rem(me, dests)]
-
-        parts = n // dests
-        pltpu.emit_pipeline(
-            qkv_body,
-            grid=(3, parts),
-            in_specs=[pl.BlockSpec((width, QKV_TILE), lambda t, p: (0, t * parts + p))],
-            out_specs=[
-                pl.BlockSpec((1, nb, dests, heads, seq_dev, head_dim), lambda t, p: (t, chunk, p, 0, 0, 0))
-            ],
-        )(w_qkv, send)
-        for step in range(1, n):
-            put(chunk, peer(step), me).start()
-        put_own(chunk).start()
+                @pl.when(chunk > 0)
+                def _():
+                    put_own(chunk - 1, kind).wait()
+
+                own[kind] = out_buf[slot, :, lax.rem(me, dests)]
+                put_own(chunk, kind).start()
+
+            @pl.when(step == 0)
+            def _():
+                pl.semaphore_wait(barrier, n - 1)
+
+            @pl.when(step > 0)
+            def _():
+                send_block(step - 1)
+
+        send_block(N_CHUNKS * blocks - 1)
+        for kind in range(3):
+            put_own(N_CHUNKS - 1, kind).wait()
+
+    pl.run_scoped(
+        qkv_phase,
+        pltpu.VMEM((rows, width), BF16),
+        pltpu.VMEM((rows, width), BF16),
+        pltpu.VMEM((2, width, QKV_HEADS, head_dim), BF16),
+        pltpu.VMEM((blocks, width, QKV_HEADS * head_dim), BF16),
+        pltpu.VMEM((rows, QKV_HEADS * head_dim), F32),
+        pltpu.VMEM((2, nb, dests, heads, seq_dev, head_dim), BF16),
+        pltpu.VMEM((3, nb, heads, seq_dev, head_dim), BF16),
+    )
 
     @pl.loop(0, N_CHUNKS)
     def _(chunk):
@@ -219,12 +279,9 @@
         def _():
             pltpu.make_async_copy(acc, resid_hbm, out_sem).start()
 
-        @pl.when(chunk == 0)
-        def _():
-            put_own(N_CHUNKS - 1).wait()
-
         for step in range(1, n):
-            put(chunk, me, peer(step)).wait_recv()
+            for kind in range(3):
+                put(chunk, kind, me, peer(step)).wait_recv()
 
         @pl.when(chunk > 0)
         def _():
@@ -262,7 +319,8 @@
     @pl.loop(0, N_CHUNKS)
     def _(chunk):
         for step in range(1, n):
-            put(chunk, peer(step), me).wait_send()
+            for kind in range(3):
+                put(chunk, kind, peer(step), me).wait_send()
             put_ctx(chunk, peer(step), me).wait_send()
             put_ctx(chunk, me, peer(step)).wait_recv()
 
@@ -292,7 +350,6 @@
         ffn = w_up.shape[1]
         q_pos = lax.axis_index("sp") * seq_dev + jnp.arange(seq_dev)
         cos_t, sin_t = rope_tables(q_pos, head_dim)
-        w_cols = w_qkv.transpose(0, 2, 1, 3).reshape(width, -1)
         row = lambda p: p.reshape(1, width)
         anywhere = pl.BlockSpec(memory_space=pl.ANY)
         vmem = pl.BlockSpec(memory_space=pltpu.VMEM)
@@ -309,23 +366,21 @@
             in_specs=[anywhere] + [vmem] * 6 + [anywhere] * 3,
             out_specs=[anywhere] * 5,
             scratch_shapes=[
-                pltpu.VMEM((nb * seq_dev, width), BF16),
-                pltpu.VMEM((nb * seq_dev, width), BF16),
                 pltpu.VMEM((rows, width), BF16),
                 pltpu.VMEM((rows, width), F32),
-                pltpu.VMEM((nb * seq_dev, QKV_TILE), F32),
-                pltpu.VMEM((3, nb, heads, seq_dev, head_dim), BF16),
                 pltpu.VMEM((nb, heads, seq_dev, head_dim), BF16),
                 pltpu.SemaphoreType.DMA,
                 pltpu.SemaphoreType.DMA((2,)),
+                pltpu.SemaphoreType.DMA((2,)),
+                pltpu.SemaphoreType.DMA((4,)),
                 pltpu.SemaphoreType.DMA,
+                pltpu.SemaphoreType.DMA((N_CHUNKS, 3, n)),
+                pltpu.SemaphoreType.DMA((N_CHUNKS, 3, n)),
                 pltpu.SemaphoreType.DMA((N_CHUNKS, n)),
                 pltpu.SemaphoreType.DMA((N_CHUNKS, n)),
-                pltpu.SemaphoreType.DMA((N_CHUNKS, n)),
-                pltpu.SemaphoreType.DMA((N_CHUNKS, n)),
             ],
             compiler_params=pltpu.CompilerParams(
-                collective_id=0, has_side_effects=True, vmem_limit_bytes=60 * 2**20
+                collective_id=0, has_side_effects=True, vmem_limit_bytes=63 * 2**20
             ),
             cost_estimate=pl.CostEstimate(flops=flops, bytes_accessed=3 * 10**8, transcendentals=10**7),
             name="layer",
@@ -337,16 +392,17 @@
             row(ln_attn_b),
             row(ln_mlp_w),
             row(ln_mlp_b),
-            w_cols,
+            w_qkv.transpose(0, 2, 1, 3),
             w_up,
             w_down,
         )
         cache = jax.ShapeDtypeStruct((n_batch, heads, n, seq_dev, head_dim), BF16)
+        nb = 1
         block = nb * seq_dev
         cache_block = (nb, heads, n, seq_dev, head_dim)
         y_out, k_cache, v_cache = pl.pallas_call(
             out_kernel,
-            grid=(N_CHUNKS,),
+            grid=(n_batch // nb,),
             out_shape=[jax.ShapeDtypeStruct((rows, width), BF16), cache, cache],
             in_specs=[
                 pl.BlockSpec((nb, n, heads, seq_dev, head_dim), lambda i: (i, 0, 0, 0, 0)),

time: 355 us -> 323 us (0.910)
  local copies, waits for them, and re-layouts: 25.6 us -> 0 us
  Pallas kernels: 325 us -> 319 us
    unnamed x1 -> x0, local copies, waits for them, and re-layouts: 25.6 us -> none
    pallas_call x1, Pallas kernels: 299 us -> 293 us  [local_layer(): pl.pallas_call(functools.partial(layer_kernel, n), out_shape=[jax.ShapeDt...]
where the time goes in v2:
time: 323 us; the launch traced here: 321 us
  Pallas kernels  319 us (99%)
    pallas_call x1, Pallas kernels, local_layer(): pl.pallas_call(functools.partial(layer_kernel, n), out_shape=[jax.ShapeDt...  293 us
    pallas_call x1, Pallas kernels, local_layer(): pl.pallas_call(out_kernel, grid=(n_batch // nb,), out_shape=[jax.ShapeDty...  26.3 us

profile of v2, /device:TPU:27, one launch (start us, length us, event | category | flops | bytes accessed | tf_op | source)
XLA Modules:
  0.0 320.9 jit_solution(5748525947430268189)
XLA Ops:
  0.7 0.3 fusion
  1.0 0.8 pad_maximum_fusion
  1.7 292.8 %layer.1 = (f32[1536,2048]{1,0:T(8,128)}, bf16[3,12,2,8,128,128]{5,4,3,2,1,0:T(8,128)(2,1)}, bf16[12,8,2,128,128]{4,3,2,1,0:T(8,128)(2,1)}, bf16[3,12,8,2,128,12...) custom-call(bf16[1536,2048]{1,0:T(8,128)(2,1)} %bitcast.10, f32[128,128]{1,0:T(8,128)} %get-tuple-element.18.cos_ref, ...), custom_call_target="tpu_custom_call" | custom-call | flops 154618822656 | bytes 300000000 | tf_op jit(solution)/shard_map/layer/pallas_call | solution.py:357
  294.5 26.3 %out.1 = (bf16[1536,2048]{1,0:T(8,128)(2,1)}, bf16[12,2,8,128,128]{4,3,2,1,0:T(8,128)(2,1)}, bf16[12,2,8,128,128]{4,3,2,1,0:T(8,128)(2,1)}) custom-call(bf16[12,8,2,128,128]{4,3,2,1,0:T(8,128)(2,1)} %get-tuple-element.9.ctx_ref, bf16[2048,2048]{1,0:T(8,128)(2,1)} %w_ref.1, f32[1536,2048]{1,0:T(8,128)} %get-tuple-element.10.resid_ref, ...), custom_call_target="tpu_custom_call" | custom-call | flops 12884901888 | bytes 60000000 | tf_op jit(solution)/shard_map/out/pallas_call | solution.py:403
  (2 shorter events, 0.0 us)

commit v3 on v2

--- a/solution.py
+++ b/solution.py
@@ -63,9 +63,10 @@
     ln_mw,
     ln_mb,
     w_qkv,
+    w_out,
     w_up,
     w_down,
-    resid_hbm,
+    y_hbm,
     recv,
     ctx_recv,
     send,
@@ -255,66 +256,104 @@
         pltpu.VMEM((3, nb, heads, seq_dev, head_dim), BF16),
     )
 
-    @pl.loop(0, N_CHUNKS)
-    def _(chunk):
-        def mlp_body(up_ref, down_ref):
-            blocks = n_batch * seq_dev // 512
-            for r in range(blocks):
-                rs = pl.ds(r * 512, 512)
-                up = jnp.dot(h_mlp[rs, :], up_ref[...], preferred_element_type=F32)
-                hid = (0.5 * up * (1.0 + lax.erf(up * 0.5**0.5))).astype(BF16)
-                acc[rs, :] += jnp.dot(hid, down_ref[...], preferred_element_type=F32)
-
-        steps = ffn // UP_TILE // N_CHUNKS
-        pltpu.emit_pipeline(
-            mlp_body,
-            grid=(steps,),
-            in_specs=[
-                pl.BlockSpec((width, UP_TILE), lambda f: (0, chunk * steps + f)),
-                pl.BlockSpec((UP_TILE, width), lambda f: (chunk * steps + f, 0)),
-            ],
-        )(w_up, w_down)
-
-        @pl.when(chunk == N_CHUNKS - 1)
-        def _():
-            pltpu.make_async_copy(acc, resid_hbm, out_sem).start()
-
-        for step in range(1, n):
-            for kind in range(3):
-                put(chunk, kind, me, peer(step)).wait_recv()
-
-        @pl.when(chunk > 0)
-        def _():
-            put_own_ctx(chunk - 1).wait()
-
-        def attn_body(q_ref, k_ref, v_ref, o_ref):
-            b, h = pl.program_id(0), pl.program_id(1)
-            flat = lambda ref: ref[...].reshape(n * seq_dev, head_dim)
-            per = Q_TILE // seq_dev
-
-            def write(i, out):
-                o_ref[0, i * per : (i + 1) * per, 0] = out.reshape(per, seq_dev, head_dim)
-
-            causal_head(flat(q_ref), flat(k_ref), flat(v_ref), write)
-            own_ctx[b, h] = o_ref[0, me, 0]
-
-        spec = lambda t: pl.BlockSpec(
-            (1, 1, 1, n, seq_dev, head_dim), lambda b, h: (t, chunk * nb + b, h, 0, 0, 0)
-        )
-        pltpu.emit_pipeline(
-            attn_body,
-            grid=(nb, heads),
-            in_specs=[spec(0), spec(1), spec(2)],
-            out_specs=[
-                pl.BlockSpec((1, n, 1, seq_dev, head_dim), lambda b, h: (chunk * nb + b, 0, h, 0, 0))
-            ],
-        )(recv, recv, recv, ctx_send)
-        for step in range(1, n):
-            put_ctx(chunk, peer(step), me).start()
-        put_own_ctx(chunk).start()
-
-    put_own_ctx(N_CHUNKS - 1).wait()
-    pltpu.make_async_copy(acc, resid_hbm, out_sem).wait()
+    def rest(w_buf, ctx_buf, ctx_rows, y_buf):
+        def get_w_out():
+            return pltpu.make_async_copy(w_out, w_buf, w_sem.at[0])
+
+        def put_y(chunk):
+            return pltpu.make_async_copy(y_buf, y_hbm.at[pl.ds(chunk * rows, rows)], out_sem)
+
+        get_w_out().start()
+
+        @pl.loop(0, N_CHUNKS)
+        def _(chunk):
+            def mlp_body(up_ref, down_ref):
+                for r in range(n_batch * seq_dev // 512):
+                    rs = pl.ds(r * 512, 512)
+                    up = jnp.dot(h_mlp[rs, :], up_ref[...], preferred_element_type=F32)
+                    hid = (0.5 * up * (1.0 + lax.erf(up * 0.5**0.5))).astype(BF16)
+                    acc[rs, :] += jnp.dot(hid, down_ref[...], preferred_element_type=F32)
+
+            steps = ffn // UP_TILE // N_CHUNKS
+            pltpu.emit_pipeline(
+                mlp_body,
+                grid=(steps,),
+                in_specs=[
+                    pl.BlockSpec((width, UP_TILE), lambda f: (0, chunk * steps + f)),
+                    pl.BlockSpec((UP_TILE, width), lambda f: (chunk * steps + f, 0)),
+                ],
+            )(w_up, w_down)
+
+            for step in range(1, n):
+                for kind in range(3):
+                    put(chunk, kind, me, peer(step)).wait_recv()
+
+            @pl.when(chunk > 0)
+            def _():
+                put_own_ctx(chunk - 1).wait()
+
+            def attn_body(q_ref, k_ref, v_ref, o_ref):
+                b, h = pl.program_id(0), pl.program_id(1)
+                flat = lambda ref: ref[...].reshape(n * seq_dev, head_dim)
+                per = Q_TILE // seq_dev
+
+                def write(i, out):
+                    o_ref[0, i * per : (i + 1) * per, 0] = out.reshape(per, seq_dev, head_dim)
+
+                causal_head(flat(q_ref), flat(k_ref), flat(v_ref), write)
+                own_ctx[b, h] = o_ref[0, me, 0]
+
+            spec = lambda t: pl.BlockSpec(
+                (1, 1, 1, n, seq_dev, head_dim), lambda b, h: (t, chunk * nb + b, h, 0, 0, 0)
+            )
+            pltpu.emit_pipeline(
+                attn_body,
+                grid=(nb, heads),
+                in_specs=[spec(0), spec(1), spec(2)],
+                out_specs=[
+                    pl.BlockSpec((1, n, 1, seq_dev, head_dim), lambda b, h: (chunk * nb + b, 0, h, 0, 0))
+                ],
+            )(recv, recv, recv, ctx_send)
+            for step in range(1, n):
+                put_ctx(chunk, peer(step), me).start()
+            put_own_ctx(chunk).start()
+
+        put_own_ctx(N_CHUNKS - 1).wait()
+        get_w_out().wait()
+
+        @pl.loop(0, N_CHUNKS)
+        def _(chunk):
+            for step in range(1, n):
+                put_ctx(chunk, me, peer(step)).wait_recv()
+            get_ctx = pltpu.make_async_copy(ctx_recv.at[pl.ds(chunk * nb, nb)], ctx_buf, x_sem)
+            get_ctx.start()
+            get_ctx.wait()
+            for b in range(nb):
+                for s in range(n):
+                    for h in range(heads):
+                        col = (s * heads + h) * head_dim
+                        ctx_rows[b * seq_dev : (b + 1) * seq_dev, col : col + head_dim] = ctx_buf[b, s, h]
+
+            @pl.when(chunk > 0)
+            def _():
+                put_y(chunk - 1).wait()
+
+            g = pl.ds(pl.multiple_of(chunk * rows, rows), rows)
+            for c in range(0, width, 1024):
+                cs = slice(c, c + 1024)
+                attn = jnp.dot(ctx_rows[...], w_buf[:, cs], preferred_element_type=F32)
+                y_buf[:, cs] = (acc[g, cs] + attn).astype(BF16)
+            put_y(chunk).start()
+
+        put_y(N_CHUNKS - 1).wait()
+
+    pl.run_scoped(
+        rest,
+        pltpu.VMEM((width, width), BF16),
+        pltpu.VMEM((nb, n, heads, seq_dev, head_dim), BF16),
+        pltpu.VMEM((rows, width), BF16),
+        pltpu.VMEM((rows, width), BF16),
+    )
 
     @pl.loop(0, N_CHUNKS)
     def _(chunk):
@@ -322,20 +361,6 @@
             for kind in range(3):
                 put(chunk, kind, peer(step), me).wait_send()
             put_ctx(chunk, peer(step), me).wait_send()
-            put_ctx(chunk, me, peer(step)).wait_recv()
-
-
-def out_kernel(ctx_ref, w_ref, resid_ref, k_in, v_in, y_ref, k_out, v_out, rows_ref):
-    nb, n, heads, seq_dev, head_dim = ctx_ref.shape
-    for b in range(nb):
-        for s in range(n):
-            for h in range(heads):
-                col = (s * heads + h) * head_dim
-                rows_ref[b * seq_dev : (b + 1) * seq_dev, col : col + head_dim] = ctx_ref[b, s, h]
-    attn = jnp.dot(rows_ref[...], w_ref[...], preferred_element_type=F32)
-    y_ref[...] = (resid_ref[...] + attn).astype(BF16)
-    k_out[...] = k_in[0]
-    v_out[...] = v_in[0]
 
 
 def solution(mesh):
@@ -354,16 +379,16 @@
         anywhere = pl.BlockSpec(memory_space=pl.ANY)
         vmem = pl.BlockSpec(memory_space=pltpu.VMEM)
         flops = 2 * rows * width * (3 * width + 2 * ffn) + 2 * rows * n * seq_dev * width * 2
-        resid, recv, ctx_recv, _, _ = pl.pallas_call(
+        y_out, recv, _, _, _ = pl.pallas_call(
             functools.partial(layer_kernel, n),
             out_shape=[
-                jax.ShapeDtypeStruct((rows, width), F32),
+                jax.ShapeDtypeStruct((rows, width), BF16),
                 jax.ShapeDtypeStruct((3, n_batch, heads, n, seq_dev, head_dim), BF16),
                 jax.ShapeDtypeStruct((n_batch, n, heads, seq_dev, head_dim), BF16),
                 jax.ShapeDtypeStruct((3, n_batch, n, heads, seq_dev, head_dim), BF16),
                 jax.ShapeDtypeStruct((n_batch, n, heads, seq_dev, head_dim), BF16),
             ],
-            in_specs=[anywhere] + [vmem] * 6 + [anywhere] * 3,
+            in_specs=[anywhere] + [vmem] * 6 + [anywhere] * 4,
             out_specs=[anywhere] * 5,
             scratch_shapes=[
                 pltpu.VMEM((rows, width), BF16),
@@ -393,38 +418,12 @@
             row(ln_mlp_w),
             row(ln_mlp_b),
             w_qkv.transpose(0, 2, 1, 3),
+            w_out,
             w_up,
             w_down,
         )
-        cache = jax.ShapeDtypeStruct((n_batch, heads, n, seq_dev, head_dim), BF16)
-        nb = 1
-        block = nb * seq_dev
-        cache_block = (nb, heads, n, seq_dev, head_dim)
-        y_out, k_cache, v_cache = pl.pallas_call(
-            out_kernel,
-            grid=(n_batch // nb,),
-            out_shape=[jax.ShapeDtypeStruct((rows, width), BF16), cache, cache],
-            in_specs=[
-                pl.BlockSpec((nb, n, heads, seq_dev, head_dim), lambda i: (i, 0, 0, 0, 0)),
-                pl.BlockSpec((width, width), lambda i: (0, 0)),
-                pl.BlockSpec((block, width), lambda i: (i, 0)),
-                pl.BlockSpec((1, *cache_block), lambda i: (1, i, 0, 0, 0, 0)),
-                pl.BlockSpec((1, *cache_block), lambda i: (2, i, 0, 0, 0, 0)),
-            ],
-            out_specs=[
-                pl.BlockSpec((block, width), lambda i: (i, 0)),
-                pl.BlockSpec(cache_block, lambda i: (i, 0, 0, 0, 0)),
-                pl.BlockSpec(cache_block, lambda i: (i, 0, 0, 0, 0)),
-            ],
-            scratch_shapes=[pltpu.VMEM((block, width), BF16)],
-            compiler_params=pltpu.CompilerParams(vmem_limit_bytes=60 * 2**20),
-            cost_estimate=pl.CostEstimate(
-                flops=2 * rows * width * width, bytes_accessed=6 * 10**7, transcendentals=0
-            ),
-            name="out",
-        )(ctx_recv, w_out, resid, recv, recv)
         shape = (n_batch, heads, n * seq_dev, head_dim)
-        return y_out.reshape(x_blk.shape), k_cache.reshape(shape), v_cache.reshape(shape)
+        return y_out.reshape(x_blk.shape), recv[1].reshape(shape), recv[2].reshape(shape)
 
     act_spec, cache_spec = P("dp", "sp", None), P("dp", "sp", None, None)
     return jax.shard_map(

time: 323 us -> 316 us (0.978)
  Pallas kernels: 319 us -> 298 us
  local copies, waits for them, and re-layouts: 0 us -> 13.5 us
    pallas_call x1 -> x0, Pallas kernels: 26.3 us -> none  [local_layer(): pl.pallas_call(out_kernel, grid=(n_batch // nb,), out_shape=[jax.ShapeDty...]
    slice x0 -> x1, local copies, waits for them, and re-layouts: none -> 10.8 us  [local_layer(): recv[2].reshape(shape)]
    pallas_call x1, Pallas kernels: 293 us -> 298 us  [local_layer(): pl.pallas_call(functools.partial(layer_kernel, n), out_shape=[jax.ShapeDt...]
where the time goes in v3:
time: 316 us; the launch traced here: 313 us
  Pallas kernels  298 us (94%)
  local copies, waits for them, and re-layouts  13.5 us (4%)
    pallas_call x1, Pallas kernels, local_layer(): pl.pallas_call(functools.partial(layer_kernel, n), out_shape=[jax.ShapeDt...  298 us
    slice x1, local copies, waits for them, and re-layouts, local_layer(): recv[2].reshape(shape)  10.8 us

profile of v3, /device:TPU:27, one launch (start us, length us, event | category | flops | bytes accessed | tf_op | source)
XLA Modules:
  0.0 313.4 jit_solution(10684836825893713050)
XLA Ops:
  0.7 0.3 fusion
  1.0 0.8 pad_maximum_fusion
  1.7 298.1 %layer.1 = (bf16[1536,2048]{1,0:T(8,128)(2,1)}, bf16[3,12,2,8,128,128]{5,4,3,2,1,0:T(8,128)(2,1)}, bf16[12,8,2,128,128]{4,3,2,1,0:T(8,128)(2,1)}, bf16[3,12,8,2,...) custom-call(bf16[1536,2048]{1,0:T(8,128)(2,1)} %bitcast.13, f32[128,128]{1,0:T(8,128)} %get-tuple-element.12.cos_ref, ...), custom_call_target="tpu_custom_call" | custom-call | flops 154618822656 | bytes 300000000 | tf_op jit(solution)/shard_map/layer/pallas_call | solution.py:382
  299.9 0.0 copy-start
  299.9 10.8 %fusion.1 = (bf16[1,12,2,8,128,128]{5,4,3,2,1,0:T(8,128)(2,1)}, bf16[1,12,2,8,128,128]{5,4,3,2,1,0:T(8,128)(2,1)}) fusion(bf16[3,12,2,8,128,128]{5,4,3,2,1,0:T(8,128)(2,1)} %get-tuple-element.6), kind=kLoop, calls=%fused_computation.7 | loop fusion | bytes 25165824 | tf_op jit(solution)/shard_map/slice | solution.py:426
  310.7 0.0 copy-done
  310.7 2.7 copy.13
  (2 shorter events, 0.0 us)
Async XLA Ops:
  299.9 10.8 %copy-start = (bf16[1536,2048]{1,0:T(8,128)(2,1)S(1)}, bf16[1536,2048]{1,0:T(8,128)(2,1)}, u32[]{:S(2)}) copy-start(bf16[1536,2048]{1,0:T(8,128)(2,1)} %get-tuple-element.5) | copy-start | bytes 18874372

commit v4 on v3

--- a/solution.py
+++ b/solution.py
@@ -14,6 +14,8 @@
 UP_TILE = 512
 QKV_HEADS = 8
 Q_TILE = 256
+FIRST = 2
+RELAYED = 3
 F32 = jnp.float32
 BF16 = jnp.bfloat16
 
@@ -27,13 +29,14 @@
 
 
 def causal_head(q, k, v, write):
-    seq, head_dim = q.shape
+    seq, head_dim = k.shape
     scale = LOG2E * head_dim**-0.5
     rows = lax.broadcasted_iota(jnp.int32, (Q_TILE, Q_TILE), 0)
     cols = lax.broadcasted_iota(jnp.int32, (Q_TILE, Q_TILE), 1)
-    for i in range(seq // Q_TILE):
-        lo, hi = i * Q_TILE, (i + 1) * Q_TILE
-        q_i = q[lo:hi]
+    for i in range(q.shape[0] // Q_TILE):
+        q_i = q[i * Q_TILE : (i + 1) * Q_TILE]
+        lo = seq - q.shape[0] + i * Q_TILE
+        hi = lo + Q_TILE
         dims = (((1,), (1,)), ((), ()))
         diag = lax.dot_general(q_i, k[lo:hi], dims, preferred_element_type=F32)
         diag = jnp.where(cols <= rows, diag, -1e30)
@@ -71,9 +74,11 @@
     ctx_recv,
     send,
     ctx_send,
+    near,
+    ctx_near,
+    relay,
     h_mlp,
     acc,
-    own_ctx,
     x_sem,
     w_sem,
     bounce_sem,
@@ -83,6 +88,12 @@
     recv_sem,
     ctx_send_sem,
     ctx_recv_sem,
+    near_send_sem,
+    near_recv_sem,
+    ctx_near_send_sem,
+    ctx_near_recv_sem,
+    relay_recv_sem,
+    relay_send_sem,
 ):
     me = lax.axis_index("sp")
     n_batch, _, heads, seq_dev, head_dim = send.shape[1:]
@@ -119,8 +130,55 @@
             device_id_type=pl.DeviceIdType.MESH,
         )
 
-    def put_own_ctx(chunk):
-        return pltpu.make_async_copy(own_ctx, ctx_recv.at[pl.ds(chunk * nb, nb), me], own_sem.at[3])
+    def put_relay(chunk, to, slot):
+        bs = pl.ds(chunk * nb, nb)
+        return pltpu.make_async_remote_copy(
+            src_ref=ctx_send.at[bs, to],
+            dst_ref=relay.at[bs, slot],
+            send_sem=ctx_send_sem.at[chunk, to],
+            recv_sem=relay_recv_sem.at[chunk, slot],
+            device_id={"sp": to - FIRST},
+            device_id_type=pl.DeviceIdType.MESH,
+        )
+
+    def forward(chunk, slot):
+        bs = pl.ds(chunk * nb, nb)
+        return pltpu.make_async_remote_copy(
+            src_ref=relay.at[bs, slot],
+            dst_ref=ctx_recv.at[bs, 2 * FIRST + slot],
+            send_sem=relay_send_sem.at[chunk, slot],
+            recv_sem=ctx_recv_sem.at[chunk, 2 * FIRST + slot],
+            device_id={"sp": me + FIRST},
+            device_id_type=pl.DeviceIdType.MESH,
+        )
+
+    def put_near(chunk, kind):
+        bs = pl.ds(chunk * nb, nb)
+        return pltpu.make_async_remote_copy(
+            src_ref=send.at[kind, bs, pl.ds((1 - me) * dests, dests)],
+            dst_ref=near.at[kind, bs],
+            send_sem=near_send_sem.at[chunk, kind],
+            recv_sem=near_recv_sem.at[chunk, kind],
+            device_id={"sp": 1 - me},
+            device_id_type=pl.DeviceIdType.MESH,
+        )
+
+    def put_ctx_near(chunk):
+        bs = pl.ds(chunk * nb, nb)
+        return pltpu.make_async_remote_copy(
+            src_ref=ctx_near.at[bs, 1 - me],
+            dst_ref=ctx_recv.at[bs, pl.ds(me * dests, dests)],
+            send_sem=ctx_near_send_sem.at[chunk],
+            recv_sem=ctx_near_recv_sem.at[chunk],
+            device_id={"sp": 1 - me},
+            device_id_type=pl.DeviceIdType.MESH,
+        )
+
+    is_first = me < FIRST
+
+    def each_peer(do, lowest=0):
+        for other in range(lowest, n):
+            pl.when(other != me)(functools.partial(do, other))
 
     def qkv_phase(x_buf, h_attn, w_nat, w_cols, qkv_acc, out_buf, own):
         def get_x(chunk):
@@ -148,9 +206,13 @@
             for d in range(dests):
                 to = lax.rem(block, parts) * dests + lax.rem(me + d, dests)
 
-                @pl.when(to != me)
+                @pl.when((to != me) & jnp.logical_not(is_first & (block < parts)))
                 def _():
                     put(step // blocks, block // parts, to, me).start()
+
+            @pl.when(is_first & (lax.rem(block, parts) == 1 - me))
+            def _():
+                put_near(step // blocks, block // parts).start()
 
         get_x(0).start()
         get_w(0).start()
@@ -256,7 +318,14 @@
         pltpu.VMEM((3, nb, heads, seq_dev, head_dim), BF16),
     )
 
-    def rest(w_buf, ctx_buf, ctx_rows, y_buf):
+    def rest(w_buf, ctx_buf, ctx_rows, y_buf, both, own_ctx, own_near):
+        def put_own_ctx(chunk):
+            return pltpu.make_async_copy(own_ctx, ctx_recv.at[pl.ds(chunk * nb, nb), me], own_sem.at[3])
+
+        def put_own_near(chunk):
+            dst = ctx_recv.at[pl.ds(chunk * nb, nb), pl.ds(me * dests, dests)]
+            return pltpu.make_async_copy(own_near, dst, own_sem.at[4])
+
         def get_w_out():
             return pltpu.make_async_copy(w_out, w_buf, w_sem.at[0])
 
@@ -284,47 +353,136 @@
                 ],
             )(w_up, w_down)
 
-            for step in range(1, n):
+            @pl.when(is_first)
+            def _():
                 for kind in range(3):
-                    put(chunk, kind, me, peer(step)).wait_recv()
-
-            @pl.when(chunk > 0)
+                    put_near(chunk, kind).wait_recv()
+
+                @pl.when(chunk > 0)
+                def _():
+                    put_own_near(chunk - 1).wait()
+
+                def near_body(q_own, k_own, v_own, q_other, k_other, v_other, o_ref):
+                    b = pl.program_id(0)
+                    for kind, (own, other) in enumerate(
+                        ((q_own, q_other), (k_own, k_other), (v_own, v_other))
+                    ):
+                        both[kind, :, :, me] = own[0, 0]
+                        both[kind, :, :, 1 - me] = other[0, 0]
+                    for d in range(dests):
+                        for h in range(heads):
+                            q, k, v = (both[t, d, h].reshape(Q_TILE, head_dim) for t in range(3))
+
+                            def write(i, out):
+                                o_ref[0, :, d, h] = out.reshape(FIRST, seq_dev, head_dim)
+
+                            causal_head(q, k, v, write)
+                    own_near[b] = o_ref[0, me]
+
+                block = (1, 1, dests, heads, seq_dev, head_dim)
+                own_spec = lambda t: pl.BlockSpec(block, lambda b: (t, chunk * nb + b, me, 0, 0, 0))
+                other_spec = lambda t: pl.BlockSpec(block, lambda b: (t, chunk * nb + b, 0, 0, 0, 0))
+                pltpu.emit_pipeline(
+                    near_body,
+                    grid=(nb,),
+                    in_specs=[own_spec(t) for t in range(3)] + [other_spec(t) for t in range(3)],
+                    out_specs=[
+                        pl.BlockSpec(
+                            (1, FIRST, dests, heads, seq_dev, head_dim),
+                            lambda b: (chunk * nb + b, 0, 0, 0, 0, 0),
+                        )
+                    ],
+                )(send, send, send, near, near, near, ctx_near)
+                put_ctx_near(chunk).start()
+                put_own_near(chunk).start()
+
+            each_peer(lambda other: put(chunk, 0, me, other).wait_recv(), FIRST)
+            each_peer(lambda other: put(chunk, 1, me, other).wait_recv())
+            each_peer(lambda other: put(chunk, 2, me, other).wait_recv())
+
+            @pl.when((chunk > 0) & jnp.logical_not(is_first))
             def _():
                 put_own_ctx(chunk - 1).wait()
 
             def attn_body(q_ref, k_ref, v_ref, o_ref):
                 b, h = pl.program_id(0), pl.program_id(1)
-                flat = lambda ref: ref[...].reshape(n * seq_dev, head_dim)
+                flat = lambda ref: ref[...].reshape(-1, head_dim)
                 per = Q_TILE // seq_dev
 
                 def write(i, out):
                     o_ref[0, i * per : (i + 1) * per, 0] = out.reshape(per, seq_dev, head_dim)
 
                 causal_head(flat(q_ref), flat(k_ref), flat(v_ref), write)
-                own_ctx[b, h] = o_ref[0, me, 0]
-
-            spec = lambda t: pl.BlockSpec(
-                (1, 1, 1, n, seq_dev, head_dim), lambda b, h: (t, chunk * nb + b, h, 0, 0, 0)
+
+                @pl.when(jnp.logical_not(is_first))
+                def _():
+                    own_ctx[b, h] = o_ref[0, me - FIRST, 0]
+
+            later = n - FIRST
+            spec = lambda count: pl.BlockSpec(
+                (1, 1, count, seq_dev, head_dim), lambda b, h: (chunk * nb + b, h, 0, 0, 0)
             )
             pltpu.emit_pipeline(
                 attn_body,
                 grid=(nb, heads),
-                in_specs=[spec(0), spec(1), spec(2)],
+                in_specs=[spec(later), spec(n), spec(n)],
                 out_specs=[
-                    pl.BlockSpec((1, n, 1, seq_dev, head_dim), lambda b, h: (chunk * nb + b, 0, h, 0, 0))
+                    pl.BlockSpec((1, later, 1, seq_dev, head_dim), lambda b, h: (chunk * nb + b, 0, h, 0, 0))
                 ],
-            )(recv, recv, recv, ctx_send)
-            for step in range(1, n):
-                put_ctx(chunk, peer(step), me).start()
-            put_own_ctx(chunk).start()
-
-        put_own_ctx(N_CHUNKS - 1).wait()
+            )(
+                recv.at[0, :, :, pl.ds(FIRST, later)],
+                recv.at[1],
+                recv.at[2],
+                ctx_send.at[:, pl.ds(FIRST, later)],
+            )
+            relays = (me // FIRST == 2) & (chunk < RELAYED)
+
+            def send_ctx(other):
+                if other // FIRST == 1:
+
+                    @pl.when(relays)
+                    def _():
+                        put_relay(chunk, other, me - 2 * FIRST).start()
+
+                    @pl.when(jnp.logical_not(relays))
+                    def _():
+                        put_ctx(chunk, other, me).start()
+
+                else:
+                    put_ctx(chunk, other, me).start()
+
+            each_peer(send_ctx, FIRST)
+
+            @pl.when(jnp.logical_not(is_first))
+            def _():
+                put_own_ctx(chunk).start()
+
+        @pl.when(is_first)
+        def _():
+            put_own_near(N_CHUNKS - 1).wait()
+
+        @pl.when(jnp.logical_not(is_first))
+        def _():
+            put_own_ctx(N_CHUNKS - 1).wait()
+
         get_w_out().wait()
 
         @pl.loop(0, N_CHUNKS)
         def _(chunk):
-            for step in range(1, n):
-                put_ctx(chunk, me, peer(step)).wait_recv()
+            @pl.when(is_first)
+            def _():
+                @pl.when(chunk < RELAYED)
+                def _():
+                    for slot in range(FIRST):
+                        put_relay(chunk, me + FIRST, slot).wait_recv()
+                        forward(chunk, slot).start()
+
+                put_ctx_near(chunk).wait_recv()
+
+            @pl.when(jnp.logical_not(is_first))
+            def _():
+                each_peer(lambda other: put_ctx(chunk, me, other).wait_recv())
+
             get_ctx = pltpu.make_async_copy(ctx_recv.at[pl.ds(chunk * nb, nb)], ctx_buf, x_sem)
             get_ctx.start()
             get_ctx.wait()
@@ -353,14 +511,34 @@
         pltpu.VMEM((nb, n, heads, seq_dev, head_dim), BF16),
         pltpu.VMEM((rows, width), BF16),
         pltpu.VMEM((rows, width), BF16),
+        pltpu.VMEM((3, dests, heads, FIRST, seq_dev, head_dim), BF16),
+        pltpu.VMEM((nb, heads, seq_dev, head_dim), BF16),
+        pltpu.VMEM((nb, dests, heads, seq_dev, head_dim), BF16),
     )
 
     @pl.loop(0, N_CHUNKS)
     def _(chunk):
-        for step in range(1, n):
+        def sent(other):
+            put(chunk, 1, other, me).wait_send()
+            put(chunk, 2, other, me).wait_send()
+
+        each_peer(sent)
+        each_peer(lambda other: put_ctx(chunk, other, me).wait_send(), FIRST)
+
+        @pl.when(is_first)
+        def _():
             for kind in range(3):
-                put(chunk, kind, peer(step), me).wait_send()
-            put_ctx(chunk, peer(step), me).wait_send()
+                put_near(chunk, kind).wait_send()
+            put_ctx_near(chunk).wait_send()
+
+            @pl.when(chunk < RELAYED)
+            def _():
+                for slot in range(FIRST):
+                    forward(chunk, slot).wait_send()
+
+        @pl.when(jnp.logical_not(is_first))
+        def _():
+            each_peer(lambda other: put(chunk, 0, other, me).wait_send())
 
 
 def solution(mesh):
@@ -372,6 +550,7 @@
         heads = groups // n
         nb = n_batch // N_CHUNKS
         rows = n_batch * seq_dev
+        dests = QKV_HEADS // heads
         ffn = w_up.shape[1]
         q_pos = lax.axis_index("sp") * seq_dev + jnp.arange(seq_dev)
         cos_t, sin_t = rope_tables(q_pos, head_dim)
@@ -379,7 +558,7 @@
         anywhere = pl.BlockSpec(memory_space=pl.ANY)
         vmem = pl.BlockSpec(memory_space=pltpu.VMEM)
         flops = 2 * rows * width * (3 * width + 2 * ffn) + 2 * rows * n * seq_dev * width * 2
-        y_out, recv, _, _, _ = pl.pallas_call(
+        y_out, recv, *_ = pl.pallas_call(
             functools.partial(layer_kernel, n),
             out_shape=[
                 jax.ShapeDtypeStruct((rows, width), BF16),
@@ -387,22 +566,30 @@
                 jax.ShapeDtypeStruct((n_batch, n, heads, seq_dev, head_dim), BF16),
                 jax.ShapeDtypeStruct((3, n_batch, n, heads, seq_dev, head_dim), BF16),
                 jax.ShapeDtypeStruct((n_batch, n, heads, seq_dev, head_dim), BF16),
+                jax.ShapeDtypeStruct((3, n_batch, dests, heads, seq_dev, head_dim), BF16),
+                jax.ShapeDtypeStruct((n_batch, FIRST, dests, heads, seq_dev, head_dim), BF16),
+                jax.ShapeDtypeStruct((n_batch, FIRST, heads, seq_dev, head_dim), BF16),
             ],
             in_specs=[anywhere] + [vmem] * 6 + [anywhere] * 4,
-            out_specs=[anywhere] * 5,
+            out_specs=[anywhere] * 8,
             scratch_shapes=[
                 pltpu.VMEM((rows, width), BF16),
                 pltpu.VMEM((rows, width), F32),
-                pltpu.VMEM((nb, heads, seq_dev, head_dim), BF16),
                 pltpu.SemaphoreType.DMA,
                 pltpu.SemaphoreType.DMA((2,)),
                 pltpu.SemaphoreType.DMA((2,)),
-                pltpu.SemaphoreType.DMA((4,)),
+                pltpu.SemaphoreType.DMA((5,)),
                 pltpu.SemaphoreType.DMA,
                 pltpu.SemaphoreType.DMA((N_CHUNKS, 3, n)),
                 pltpu.SemaphoreType.DMA((N_CHUNKS, 3, n)),
                 pltpu.SemaphoreType.DMA((N_CHUNKS, n)),
                 pltpu.SemaphoreType.DMA((N_CHUNKS, n)),
+                pltpu.SemaphoreType.DMA((N_CHUNKS, 3)),
+                pltpu.SemaphoreType.DMA((N_CHUNKS, 3)),
+                pltpu.SemaphoreType.DMA((N_CHUNKS,)),
+                pltpu.SemaphoreType.DMA((N_CHUNKS,)),
+                pltpu.SemaphoreType.DMA((N_CHUNKS, FIRST)),
+                pltpu.SemaphoreType.DMA((N_CHUNKS, FIRST)),
             ],
             compiler_params=pltpu.CompilerParams(
                 collective_id=0, has_side_effects=True, vmem_limit_bytes=63 * 2**20

time: 316 us -> 364 us (1.15)
  Pallas kernels: 298 us -> 348 us
    pallas_call x1, Pallas kernels: 298 us -> 348 us  [local_layer(): pl.pallas_call(functools.partial(layer_kernel, n), out_shape=[jax.ShapeDt...]
where the time goes in v4:
time: 364 us; the launch traced here: 363 us
  Pallas kernels  348 us (96%)
  local copies, waits for them, and re-layouts  13.5 us (4%)
    pallas_call x1, Pallas kernels, local_layer(): pl.pallas_call(functools.partial(layer_kernel, n), out_shape=[jax.ShapeDt...  348 us
    slice x1, local copies, waits for them, and re-layouts, local_layer(): recv[2].reshape(shape)  10.8 us

profile of v4, /device:TPU:27, one launch (start us, length us, event | category | flops | bytes accessed | tf_op | source)
XLA Modules:
  0.0 363.3 jit_solution(5199824121608666662)
XLA Ops:
  0.7 0.3 fusion
  1.0 0.8 pad_maximum_fusion
  1.7 348.0 %layer.1 = (bf16[1536,2048]{1,0:T(8,128)(2,1)}, bf16[3,12,2,8,128,128]{5,4,3,2,1,0:T(8,128)(2,1)}, bf16[12,8,2,128,128]{4,3,2,1,0:T(8,128)(2,1)}, bf16[3,12,8,2,...) custom-call(bf16[1536,2048]{1,0:T(8,128)(2,1)} %bitcast.13, ...), custom_call_target="tpu_custom_call" | custom-call | flops 154618822656 | bytes 300000000 | tf_op jit(solution)/shard_map/layer/pallas_call | solution.py:561
  349.8 0.0 copy-start
  349.8 10.8 %fusion.1 = (bf16[1,12,2,8,128,128]{5,4,3,2,1,0:T(8,128)(2,1)}, bf16[1,12,2,8,128,128]{5,4,3,2,1,0:T(8,128)(2,1)}) fusion(bf16[3,12,2,8,128,128]{5,4,3,2,1,0:T(8,128)(2,1)} %get-tuple-element.6), kind=kLoop, calls=%fused_computation.7 | loop fusion | bytes 25165824 | tf_op jit(solution)/shard_map/slice | solution.py:613
  360.6 0.0 copy-done
  360.6 2.7 copy.13
  (2 shorter events, 0.0 us)
Async XLA Ops:
  349.8 10.8 %copy-start = (bf16[1536,2048]{1,0:T(8,128)(2,1)S(1)}, bf16[1536,2048]{1,0:T(8,128)(2,1)}, u32[]{:S(2)}) copy-start(bf16[1536,2048]{1,0:T(8,128)(2,1)} %get-tuple-element.5) | copy-start | bytes 18874372
